TPU v7x, 32 devices: a whole 2x2x4 slice. The times are simulated.
32 devices in a mesh: ba: 8 (over z, y), dev: 4 (over x, core).
Axes of the slice: x: 2, y: 2, z: 4, core: 2. Of those that a mesh axis runs over, the one named last changes fastest.
Arguments:
- factors: bfloat16 [16, 512, 1024], P('ba', 'dev'), may hold values from -0.1875 to 0.1875
- amplitudes: bfloat16 [64, 512, 512], P(None, 'dev'), may hold values from -0.375 to 0.375
- pair_order: int32 [64], replicated, may hold values from 0 to 63, each once
- occ_bin: int32 [8], replicated, may hold values from 0 to 127
- vir_bin: int32 [16], replicated, may hold values from 0 to 127
- levels: float32 [128], replicated, may hold values from 0.1 to 0.8
Outputs:
- update: float32 [16, 1024], P('ba', 'dev')
Inputs may be any that keep to these rules, and one draw needn't show every extreme that they name: `pair_order`: each value appears once; entry k names the ordered occupied pair (value // 8, value % 8). `occ_bin`: orbital i has energy minus levels at its bin. `vir_bin`: window virtual a has energy levels at its bin.
All inputs are finite; a program needn't handle non-finite values.
Results may differ from a plain program's by a relative error of at most 0.0029.
Values may be sent and summed in bfloat16 or wider, within the bound.
A program may use at most 64 MiB of HBM per device.

v0:
```python
import functools

import jax
import jax.numpy as jnp
from jax import lax
from jax.experimental import pallas as pl
from jax.experimental.pallas import tpu as pltpu
from jax.sharding import PartitionSpec as P

NOCC = 8
LANES = 128
MESH = pl.DeviceIdType.MESH

level_shift = 0.3


def flip_bits(index, bits):
    result = index
    bit = 1
    while bit <= bits:
        if bits & bit:
            result = result + bit - 2 * bit * ((result // bit) % 2)
        bit *= 2
    return result


def to_column(row):
    n = row.shape[1]
    rows = lax.broadcasted_iota(jnp.int32, (n, n), 0)
    lanes = lax.broadcasted_iota(jnp.int32, (n, n), 1)
    return jnp.sum(jnp.where(rows == lanes, row, jnp.zeros_like(row)), axis=1, keepdims=True)


def kernel(
    dims,
    f_hbm,
    amps_hbm,
    order_ref,
    occ_ref,
    vir_ref,
    levels_ref,
    out_ref,
    local,
    right,
    other,
    left_f32,
    left,
    raw,
    stage,
    amps,
    ints,
    flat,
    acc,
    tiles,
    parts,
    load_sem,
    own_sem,
    amp_sem,
    send_z,
    send_o,
    send_c,
    send_y,
    recv_piece,
    recv_y,
    send_f,
    recv_f,
):
    nz, ny, no, owned, cols, qs, window, pairs, virt, tile_c, amp_c = dims
    nd = no * 2
    nb = nz * owned
    total = nz * ny * nd
    split = window // nd
    ba, dev = lax.axis_index("ba"), lax.axis_index("dev")
    me = ba * nd + dev
    z, y = ba // ny, ba % ny
    outer, core = dev // 2, dev % 2
    partner_core = outer * 2 + 1 - core
    chunks = cols // amp_c
    half, half_z = window // 2, nz // 2
    mine = z // half_z
    halves = (mine, 1 - mine)

    load = pltpu.make_async_copy(f_hbm, local, load_sem)
    load.start()
    own = pltpu.make_async_copy(
        f_hbm.at[:, :, pl.ds(pl.multiple_of(z * qs, LANES), qs)], right.at[z, :, dev], own_sem
    )
    own.start()

    def amp_load(chunk):
        return pltpu.make_async_copy(
            amps_hbm.at[:, pl.ds(chunk * amp_c, amp_c), :], raw.at[chunk], amp_sem.at[chunk]
        )

    for chunk in range(chunks):
        amp_load(chunk).start()

    barrier = pltpu.get_barrier_semaphore()

    def greet(step, carry):
        there = (me + step) % total
        pl.semaphore_signal(
            barrier, inc=1, device_id=(there // nd, there % nd), device_id_type=MESH
        )
        return carry

    lax.fori_loop(1, total, greet, 0)
    load.wait()
    own.wait()
    pl.semaphore_wait(barrier, total - 1)

    def piece_copy(piece_z, row, piece_d, send, ba_to, dev_to):
        return pltpu.make_async_remote_copy(
            src_ref=right.at[piece_z, row, piece_d],
            dst_ref=right.at[piece_z, row, piece_d],
            send_sem=send,
            recv_sem=recv_piece.at[piece_z, row, piece_d],
            device_id=(ba_to, dev_to),
            device_id_type=MESH,
        )

    def await_piece(piece_z, row, piece_d):
        piece_copy(piece_z, row, piece_d, send_z.at[0, 0], ba, partner_core).wait_recv()

    pending = []
    for step in range(1, nz):
        there = flip_bits(z, step)
        for row in range(owned):
            copy = pltpu.make_async_remote_copy(
                src_ref=local.at[row, :, pl.ds(pl.multiple_of(there * qs, LANES), qs)],
                dst_ref=right.at[z, row, dev],
                send_sem=send_z.at[step, row],
                recv_sem=recv_piece.at[z, row, dev],
                device_id=(there * ny + y, dev),
                device_id_type=MESH,
            )
            copy.start()
            pending.append(copy)

    def forward(step, row):
        from_z = flip_bits(z, step)
        if step:
            await_piece(from_z, row, dev)
        for other_outer in range(1, no):
            copy = piece_copy(
                from_z,
                row,
                dev,
                send_o.at[step, row, other_outer],
                ba,
                flip_bits(outer, other_outer) * 2 + core,
            )
            copy.start()
            pending.append(copy)
        for other_y in range(1, ny):
            copy = pltpu.make_async_remote_copy(
                src_ref=right.at[from_z, row, dev],
                dst_ref=other.at[y, from_z, row],
                send_sem=send_y.at[step, row, other_y],
                recv_sem=recv_y.at[y, from_z, row],
                device_id=(z * ny + flip_bits(y, other_y), dev),
                device_id_type=MESH,
            )
            copy.start()
            pending.append(copy)
        copy = piece_copy(from_z, row, dev, send_c.at[step, row, 0], ba, partner_core)
        copy.start()
        pending.append(copy)

    def widen(source, at_y, at_z):
        for i in range(owned):
            row = (at_z * ny + at_y) * owned + i
            base = pl.multiple_of(row * (cols + 8), 8)
            for h in range(qs // LANES):
                left_f32[h, pl.ds(base, cols), :] = source[
                    i, :, h * LANES : (h + 1) * LANES
                ].astype(jnp.float32)

    def amp_chunk(chunk):
        amp_load(chunk).wait()
        pitch = amp_c + 8

        def spread(k, carry):
            base = pl.multiple_of(k * pitch, 8)
            for h in range(virt // LANES):
                stage[h, pl.ds(base, amp_c), :] = raw[
                    chunk, k, :, h * LANES : (h + 1) * LANES
                ].astype(jnp.float32)
            return carry

        lax.fori_loop(0, pairs, spread, 0, unroll=4)

        def gather(c, carry):
            for h in range(virt // LANES):
                amps[chunk * amp_c + c, :, h * LANES : (h + 1) * LANES] = stage[
                    h, pl.ds(c, pairs, stride=pitch), :
                ].astype(jnp.bfloat16)
            return carry

        lax.fori_loop(0, amp_c, gather, 0)

    def own_rows(step):
        from_z = flip_bits(z, step)
        widen(right.at[from_z, :, dev], y, from_z)

    def collect(step):
        from_z = flip_bits(z, step)
        for row in range(owned):
            for other_outer in range(1, no):
                from_d = flip_bits(outer, other_outer) * 2 + core
                await_piece(from_z, row, from_d)
                copy = piece_copy(
                    from_z, row, from_d, send_c.at[step, row, other_outer], ba, partner_core
                )
                copy.start()
                pending.append(copy)
        for other_y in range(1, ny):
            from_y = flip_bits(y, other_y)
            for row in range(owned):
                pltpu.make_async_remote_copy(
                    src_ref=right.at[from_z, row, dev],
                    dst_ref=other.at[from_y, from_z, row],
                    send_sem=send_z.at[0, 0],
                    recv_sem=recv_y.at[from_y, from_z, row],
                    device_id=(ba, partner_core),
                    device_id_type=MESH,
                ).wait_recv()
            widen(other.at[from_y, from_z], from_y, from_z)

    def finish(step):
        from_z = flip_bits(z, step)
        for row in range(owned):
            for other_outer in range(no):
                await_piece(from_z, row, flip_bits(outer, other_outer) * 2 + 1 - core)

    def turn_half(side):
        first_row = halves[side] * half * (cols + 8)

        def turn(step, carry):
            at = step * 2
            rows = pl.ds(pl.multiple_of(at * half, 2 * half), 2 * half)
            for h in range(qs // LANES):
                left[side, rows, h * LANES : (h + 1) * LANES] = jnp.concatenate(
                    [
                        left_f32[h, pl.ds(first_row + at + i, half, stride=cols + 8), :]
                        for i in range(2)
                    ],
                    axis=0,
                ).astype(jnp.bfloat16)
            return carry

        lax.fori_loop(0, cols // 2, turn, 0, unroll=4)

    block = tile_c * half
    early = [(0, 0, j) for j in range(half_z)]
    late = [(1, side, j) for side in range(2) for j in range(half_z)] + [
        (0, 1, j) for j in range(half_z)
    ]
    height_of = owned * half

    def contract(ct, jobs, base):
        for at, (a_side, b_side, j) in enumerate(jobs):
            rows = left[a_side, pl.ds(pl.multiple_of(ct * block, block), block), :]
            from_z = halves[b_side] * half_z + j
            parts_of = []
            for i in range(owned):
                side = right[from_z, i].reshape(virt, qs)
                parts_of.append(
                    lax.dot_general(
                        rows, side, (((1,), (1,)), ((), ())), preferred_element_type=jnp.float32
                    ).reshape(tile_c, half, virt)
                )
            ints[:, at * height_of : (at + 1) * height_of, :] = jnp.concatenate(
                parts_of, axis=1
            ).astype(jnp.bfloat16)
        count = len(jobs) * height_of

        def add(t, value):
            return value + lax.dot_general(
                ints[t, 0:count, :],
                amps[ct * tile_c + t],
                (((1,), (1,)), ((), ())),
                preferred_element_type=jnp.float32,
            )

        flat[base : base + count, :] += lax.fori_loop(
            0, tile_c, add, jnp.zeros((count, pairs), jnp.float32), unroll=tile_c
        )

    flat[...] = jnp.zeros_like(flat)
    done = 0
    for step in range(half_z):
        for row in range(owned):
            forward(step, row)
            upto = (step * owned + row + 1) * chunks // (half_z * owned)
            for chunk in range(done, upto):
                amp_chunk(chunk)
            done = upto
        own_rows(step)
    for step in range(half_z, nz - 1):
        for row in range(owned):
            forward(step, row)
    for step in range(half_z):
        collect(step)
    turn_half(0)
    for step in range(half_z):
        finish(step)
    for row in range(owned):
        forward(nz - 1, row)

    def early_tile(ct, carry):
        contract(ct, early, 0)
        return carry

    lax.fori_loop(0, cols // tile_c, early_tile, 0)
    for step in range(half_z, nz):
        own_rows(step)
    for step in range(half_z, nz):
        collect(step)
    turn_half(1)
    for step in range(half_z, nz):
        finish(step)
    late_base = len(early) * height_of

    def late_tile(ct, carry):
        contract(ct, late, late_base)
        return carry

    lax.fori_loop(0, cols // tile_c, late_tile, 0)
    for at, (a_side, b_side, j) in enumerate(early + late):
        for i in range(owned):
            value = flat[at * height_of + i * half : at * height_of + (i + 1) * half, :]
            acc[
                (halves[b_side] * half_z + j) * owned + i,
                pl.ds(pl.multiple_of(halves[a_side] * half, 8), half),
                0:pairs,
            ] = value
    acc[:, :, pairs : 2 * pairs] = acc[:, :, 0:pairs]

    height = owned * split
    row_at = lax.broadcasted_iota(jnp.int32, (height, 2 * pairs), 0)
    lane_at = lax.broadcasted_iota(jnp.int32, (height, 2 * pairs), 1)

    def make_tile(there):
        to_ba, to_dev = there // nd, there % nd
        to_z, to_y = to_ba // ny, to_ba % ny
        straight = jnp.zeros((height, 2 * pairs), jnp.float32)
        pieces = []
        turned = []
        for i in range(owned):
            pieces.append(acc[to_z * owned + i, pl.ds(to_dev * split, split), :])
            for a in range(split):
                row = to_dev * split + a
                owner = row // owned
                turned.append(
                    acc[(owner // ny) * owned + row % owned, pl.ds(to_ba * owned + i, 1), :]
                )
        straight = jnp.concatenate(pieces, axis=0)
        flipped = jnp.concatenate(turned, axis=0)
        same = jnp.zeros((height, 2 * pairs), jnp.int32) + to_y == y
        owner_at = (to_dev * split + row_at % split) // owned
        return jnp.where(
            lane_at < pairs,
            jnp.where(same, straight, 0.0),
            jnp.where(owner_at % ny == y, flipped, 0.0),
        )

    def tile_copy(there):
        return pltpu.make_async_remote_copy(
            src_ref=tiles.at[there],
            dst_ref=parts.at[me],
            send_sem=send_f.at[there],
            recv_sem=recv_f.at[me],
            device_id=(there // nd, there % nd),
            device_id_type=MESH,
        )

    def send_tile(step, carry):
        there = (me + step) % total
        tiles[there] = make_tile(there)
        tile_copy(there).start()
        return carry

    lax.fori_loop(1, total, send_tile, 0)
    parts[me] = make_tile(me)

    levels = to_column(levels_ref[...])
    level_at = lax.broadcasted_iota(jnp.int32, (levels.shape[0], window), 0)
    virtual = jnp.sum(
        jnp.where(level_at == vir_ref[...], levels, 0.0), axis=0, keepdims=True
    )
    level_occ = lax.broadcasted_iota(jnp.int32, (levels.shape[0], NOCC), 0)
    occupied = to_column(
        -jnp.sum(jnp.where(level_occ == occ_ref[...], levels, 0.0), axis=0, keepdims=True)
    )
    order = order_ref[...]
    first, second = order // NOCC, order % NOCC
    occ_at = lax.broadcasted_iota(jnp.int32, (NOCC, pairs), 0)
    pair_energy = jnp.sum(
        jnp.where(occ_at == first, occupied, 0.0), axis=0, keepdims=True
    ) + jnp.sum(jnp.where(occ_at == second, occupied, 0.0), axis=0, keepdims=True)
    win_row = lax.broadcasted_iota(jnp.int32, (height, window), 0)
    win_lane = lax.broadcasted_iota(jnp.int32, (height, window), 1)
    right_energy = jnp.sum(
        jnp.where(win_lane == ba * owned + win_row // split, virtual, 0.0), axis=1, keepdims=True
    )
    left_energy = jnp.sum(
        jnp.where(win_lane == dev * split + win_row % split, virtual, 0.0), axis=1, keepdims=True
    )
    denominator = right_energy + left_energy - pair_energy + level_shift
    permuter = (to_column(order) == second * NOCC + first).astype(jnp.float32)

    def arrive(step, carry):
        there = (me + step) % total
        pltpu.make_async_remote_copy(
            src_ref=tiles.at[there],
            dst_ref=parts.at[there],
            send_sem=send_f.at[there],
            recv_sem=recv_f.at[there],
            device_id=(there // nd, there % nd),
            device_id_type=MESH,
        ).wait_recv()
        return carry

    lax.fori_loop(1, total, arrive, 0)
    summed = jnp.sum(parts[...], axis=0)
    moved = jnp.dot(
        summed[:, pairs:],
        permuter,
        precision=lax.Precision.HIGHEST,
        preferred_element_type=jnp.float32,
    )
    result = (summed[:, :pairs] + moved) / denominator
    for i in range(owned):
        for a in range(split):
            out_ref[i : i + 1, a * pairs : (a + 1) * pairs] = result[
                i * split + a : i * split + a + 1, :
            ]

    for copy in pending:
        copy.wait_send()

    def sent(step, carry):
        tile_copy((me + step) % total).wait_send()
        return carry

    lax.fori_loop(1, total, sent, 0)


def per_device(nba, ndev, factors, amplitudes, pair_order, occ_bin, vir_bin, levels):
    owned, cols, fitting = factors.shape
    pairs, _, virt = amplitudes.shape
    window = owned * nba
    ny = 1
    while ny * ny * 4 <= nba:
        ny *= 2
    nz = nba // ny
    no = ndev // 2
    qs = fitting // nz
    nb = nz * owned
    split = window // ndev
    total = nba * ndev
    tile_c = min(cols, max(1, (4 << 20) // (nb * window * virt * 2)))
    amp_c = 16
    dims = (nz, ny, no, owned, cols, qs, window, pairs, virt, tile_c, amp_c)
    dma = pltpu.SemaphoreType.DMA
    vmem = pl.BlockSpec(memory_space=pltpu.VMEM)
    hbm = pl.BlockSpec(memory_space=pl.ANY)
    return pl.pallas_call(
        functools.partial(kernel, dims),
        out_shape=jax.ShapeDtypeStruct((owned, split * pairs), jnp.float32),
        in_specs=[hbm, hbm, vmem, vmem, vmem, vmem],
        out_specs=vmem,
        scratch_shapes=[
            pltpu.VMEM((owned, cols, fitting), jnp.bfloat16),
            pltpu.VMEM((nz, owned, ndev, cols, qs), jnp.bfloat16),
            pltpu.VMEM((ny, nz, owned, cols, qs), jnp.bfloat16),
            pltpu.VMEM((qs // LANES, window * (cols + 8), LANES), jnp.float32),
            pltpu.VMEM((2, cols * window // 2, qs), jnp.bfloat16),
            pltpu.VMEM((cols // amp_c, pairs, amp_c, virt), jnp.bfloat16),
            pltpu.VMEM((virt // LANES, pairs * (amp_c + 8), LANES), jnp.float32),
            pltpu.VMEM((cols, pairs, virt), jnp.bfloat16),
            pltpu.VMEM((tile_c, nb * window, virt), jnp.bfloat16),
            pltpu.VMEM((nb * window, pairs), jnp.float32),
            pltpu.VMEM((nb, window, 2 * pairs), jnp.float32),
            pltpu.VMEM((total, owned * split, 2 * pairs), jnp.float32),
            pltpu.VMEM((total, owned * split, 2 * pairs), jnp.float32),
            dma,
            dma,
            dma((cols // amp_c,)),
            dma((nz, owned)),
            dma((nz, owned, no)),
            dma((nz, owned, no)),
            dma((nz, owned, ny)),
            dma((nz, owned, ndev)),
            dma((ny, nz, owned)),
            dma((total,)),
            dma((total,)),
        ],
        compiler_params=pltpu.CompilerParams(
            collective_id=0, has_side_effects=True, vmem_limit_bytes=56 << 20
        ),
    )(
        factors,
        amplitudes,
        pair_order.reshape(1, -1),
        occ_bin.reshape(1, -1),
        vir_bin.reshape(1, -1),
        levels.reshape(1, -1),
    )


def solution(mesh):
    return jax.shard_map(
        functools.partial(per_device, mesh.shape["ba"], mesh.shape["dev"]),
        mesh=mesh,
        in_specs=(P("ba", "dev", None), P(None, "dev", None), P(), P(), P(), P()),
        out_specs=P("ba", "dev"),
        check_vma=False,
    )
```

profile of v0, /device:TPU:0, one launch (start us, length us, event | category | flops | bytes accessed | tf_op | source)
XLA Modules:
  0.0 42.7 jit_solution(18365996149714648291)
XLA Ops:
  0.0 41.4 %shard_map.64 = f32[2,256]{1,0:T(2,128)} custom-call(bf16[2,128,1024]{2,1,0:T(8,128)(2,1)} %f_hbm.1, bf16[64,128,512]{2,1,0:T(8,128)(2,1)} %amps_hbm.1, s32[1,64]{1,0:T(1,128)} %bitcast.4, s32[1,8]{1,0:T(1,128)} %bitcast.5, s32[1,16]{1,0:T(1,128)} %bitcast.6, f32[1,128]{1,0:T(1,128)} %bitcast.7), custom_call_target="tpu_custom_call" | custom-call | tf_op jit(solution)/shard_map/pallas_call | solution.py:469
  41.5 1.3 %copy.8 = f32[2,256]{1,0:T(2,128)} copy(f32[2,256]{1,0:T(2,128)} %shard_map.64) | data formatting | bytes 4096
where the time goes:
time: 42.9 us; the launch traced here: 42.7 us
  Pallas kernels  41.4 us (97%)
  local copies, waits for them, and re-layouts  1.26 us (3%)
    pallas_call x1, Pallas kernels, per_device(): pl.pallas_call(functools.partial(kernel, dims), out_shape=jax.ShapeDtypeS...  41.4 us
    unnamed x1, local copies, waits for them, and re-layouts  1.26 us

commit v1 on v0

--- a/solution.py
+++ b/solution.py
@@ -97,17 +97,15 @@
 
     barrier = pltpu.get_barrier_semaphore()
 
-    def greet(step, carry):
-        there = (me + step) % total
-        pl.semaphore_signal(
-            barrier, inc=1, device_id=(there // nd, there % nd), device_id_type=MESH
-        )
-        return carry
-
-    lax.fori_loop(1, total, greet, 0)
+    near = [(flip_bits(z, step) * ny + y, dev) for step in range(1, nz)]
+    near += [(z * ny + flip_bits(y, step), dev) for step in range(1, ny)]
+    near += [(ba, flip_bits(outer, step) * 2 + core) for step in range(1, no)]
+    near.append((ba, partner_core))
+    for there in near:
+        pl.semaphore_signal(barrier, inc=1, device_id=there, device_id_type=MESH)
     load.wait()
     own.wait()
-    pl.semaphore_wait(barrier, total - 1)
+    pl.semaphore_wait(barrier, len(near))
 
     def piece_copy(piece_z, row, piece_d, send, ba_to, dev_to):
         return pltpu.make_async_remote_copy(

time: 42.9 us -> 41.6 us (0.970)
  Pallas kernels: 41.4 us -> 40.2 us
    pallas_call x1, Pallas kernels: 41.4 us -> 40.2 us  [per_device(): pl.pallas_call(functools.partial(kernel, dims), out_shape=jax.ShapeDtypeS...]
where the time goes in v1:
time: 41.6 us; the launch traced here: 41.5 us
  Pallas kernels  40.2 us (97%)
  local copies, waits for them, and re-layouts  1.26 us (3%)
    pallas_call x1, Pallas kernels, per_device(): pl.pallas_call(functools.partial(kernel, dims), out_shape=jax.ShapeDtypeS...  40.2 us
    unnamed x1, local copies, waits for them, and re-layouts  1.26 us

profile of v1, /device:TPU:0, one launch (start us, length us, event | category | flops | bytes accessed | tf_op | source)
XLA Modules:
  0.0 41.5 jit_solution(14979658817878373883)
XLA Ops:
  0.0 40.2 %shard_map.64 = f32[2,256]{1,0:T(2,128)} custom-call(bf16[2,128,1024]{2,1,0:T(8,128)(2,1)} %f_hbm.1, bf16[64,128,512]{2,1,0:T(8,128)(2,1)} %amps_hbm.1, s32[1,64]{1,0:T(1,128)} %bitcast.4, s32[1,8]{1,0:T(1,128)} %bitcast.5, s32[1,16]{1,0:T(1,128)} %bitcast.6, f32[1,128]{1,0:T(1,128)} %bitcast.7), custom_call_target="tpu_custom_call" | custom-call | tf_op jit(solution)/shard_map/pallas_call | solution.py:467
  40.2 1.3 %copy.8 = f32[2,256]{1,0:T(2,128)} copy(f32[2,256]{1,0:T(2,128)} %shard_map.64) | data formatting | bytes 4096

commit v2 on v1

v2 whole, which is shorter than its diff:
```python
import functools

import jax
import jax.numpy as jnp
from jax import lax
from jax.experimental import pallas as pl
from jax.experimental.pallas import tpu as pltpu
from jax.sharding import PartitionSpec as P

NOCC = 8
LANES = 128
MESH = pl.DeviceIdType.MESH

level_shift = 0.3


def flip_bits(index, bits):
    result = index
    bit = 1
    while bit <= bits:
        if bits & bit:
            result = result + bit - 2 * bit * ((result // bit) % 2)
        bit *= 2
    return result


def to_column(row):
    n = row.shape[1]
    rows = lax.broadcasted_iota(jnp.int32, (n, n), 0)
    lanes = lax.broadcasted_iota(jnp.int32, (n, n), 1)
    return jnp.sum(jnp.where(rows == lanes, row, jnp.zeros_like(row)), axis=1, keepdims=True)


def kernel(
    dims,
    f_hbm,
    amps_hbm,
    order_hbm,
    occ_hbm,
    vir_hbm,
    levels_hbm,
    out_ref,
    order_ref,
    occ_ref,
    vir_ref,
    levels_ref,
    right,
    other,
    left_f32,
    left,
    raw,
    stage,
    amps,
    ints,
    flat,
    acc,
    tiles_s,
    tiles_f,
    parts_s,
    parts_f,
    own_sem,
    small_sem,
    amp_sem,
    sent_z,
    sent_x,
    sent_y,
    sent_c,
    sent_f,
    recv_z,
    recv_x,
    recv_c,
    recv_y,
    recv_f,
):
    nz, ny, no, owned, cols, qs, window, pairs, virt, amp_c, slabs = dims
    nd = no * 2
    nb = nz * owned
    total = nz * ny * nd
    split = window // nd
    wide = cols // slabs
    ba, dev = lax.axis_index("ba"), lax.axis_index("dev")
    me = ba * nd + dev
    z, y = ba // ny, ba % ny
    outer, core = dev // 2, dev % 2
    partner_core = outer * 2 + 1 - core
    chunks = cols // amp_c

    barrier = pltpu.get_barrier_semaphore()
    near = [(flip_bits(z, step) * ny + y, dev) for step in range(1, nz)]
    near += [(z * ny + flip_bits(y, step), dev) for step in range(1, ny)]
    near += [(ba, flip_bits(outer, step) * 2 + core) for step in range(1, no)]
    near.append((ba, partner_core))
    for there in near:
        pl.semaphore_signal(barrier, inc=1, device_id=there, device_id_type=MESH)

    def quarter(at_z):
        return pl.ds(pl.multiple_of(at_z * qs, LANES), qs)

    def factor_slab(slab, at_z):
        return f_hbm.at[:, pl.ds(slab * wide, wide), quarter(at_z)]

    own = pltpu.make_async_copy(f_hbm.at[:, :, quarter(z)], right.at[z, :, dev], own_sem)
    own.start()

    def amp_load(chunk):
        return pltpu.make_async_copy(
            amps_hbm.at[:, pl.ds(chunk * amp_c, amp_c), :], raw.at[chunk], amp_sem.at[chunk]
        )

    for chunk in range(chunks):
        amp_load(chunk).start()
    small = [
        pltpu.make_async_copy(source, target, small_sem.at[at])
        for at, (source, target) in enumerate(
            (
                (order_hbm, order_ref),
                (occ_hbm, occ_ref),
                (vir_hbm, vir_ref),
                (levels_hbm, levels_ref),
            )
        )
    ]
    for copy in small:
        copy.start()
    pl.semaphore_wait(barrier, len(near))

    def send(source, target, send_sem, recv_sem, ba_to, dev_to):
        copy = pltpu.make_async_remote_copy(
            src_ref=source,
            dst_ref=target,
            send_sem=send_sem,
            recv_sem=recv_sem,
            device_id=(ba_to, dev_to),
            device_id_type=MESH,
        )
        copy.start()

    def await_bytes(place, recv_sem):
        pltpu.make_async_remote_copy(
            src_ref=place,
            dst_ref=place,
            send_sem=sent_z,
            recv_sem=recv_sem,
            device_id=(ba, partner_core),
            device_id_type=MESH,
        ).wait_recv()

    def piece(slab, at_z, at_d):
        return right.at[at_z, :, at_d, pl.ds(slab * wide, wide), :]

    def to_partner(source, slab, step, at_d):
        at_z = flip_bits(z, step)
        send(source, piece(slab, at_z, at_d), sent_c, recv_c.at[min(step // 2, 1)], ba, partner_core)

    def spread(source, slab, step):
        at_z = flip_bits(z, step)
        for other_outer in range(1, no):
            send(
                source,
                piece(slab, at_z, dev),
                sent_x,
                recv_x.at[slab, step, other_outer - 1],
                ba,
                flip_bits(outer, other_outer) * 2 + core,
            )
        for other_y in range(1, ny):
            send(
                source,
                other.at[slab, other_y - 1, at_z],
                sent_y,
                recv_y.at[slab],
                z * ny + flip_bits(y, other_y),
                dev,
            )
        to_partner(source, slab, step, dev)


    def launch(slab, steps):
        for step in steps:
            at_z = flip_bits(z, step)
            send(
                factor_slab(slab, at_z),
                piece(slab, z, dev),
                sent_z,
                recv_z.at[slab, step - 1],
                at_z * ny + y,
                dev,
            )

    def from_z(slab, step):
        place = piece(slab, flip_bits(z, step), dev)
        await_bytes(place, recv_z.at[slab, step - 1])
        spread(place, slab, step)

    def from_x(slab, step):
        for other_outer in range(1, no):
            at_d = flip_bits(outer, other_outer) * 2 + core
            place = piece(slab, flip_bits(z, step), at_d)
            await_bytes(place, recv_x.at[slab, step, other_outer - 1])
            to_partner(place, slab, step, at_d)

    def from_core(steps):
        await_bytes(right.at[0 : len(steps), :, 0:no], recv_c.at[min(steps[0] // 2, 1)])

    def widen(source, row):
        base = pl.multiple_of(row * (wide + 8), 8)
        for h in range(qs // LANES):
            left_f32[h, pl.ds(base, wide), :] = source[:, h * LANES : (h + 1) * LANES].astype(
                jnp.float32
            )

    def make_left(slab):
        if ny > 1:
            await_bytes(other.at[slab, 0 : ny - 1], recv_y.at[slab])
        for at_z in range(nz):
            for i in range(owned):
                widen(
                    right.at[at_z, i, dev, pl.ds(slab * wide, wide), :],
                    (at_z * ny + y) * owned + i,
                )
                for other_y in range(1, ny):
                    at_y = flip_bits(y, other_y)
                    widen(other.at[slab, other_y - 1, at_z, i], (at_z * ny + at_y) * owned + i)

        def turn(c, carry):
            rows = pl.ds(pl.multiple_of((slab * wide + c) * window, window), window)
            for h in range(qs // LANES):
                left[rows, h * LANES : (h + 1) * LANES] = left_f32[
                    h, pl.ds(c, window, stride=wide + 8), :
                ].astype(jnp.bfloat16)
            return carry

        lax.fori_loop(0, wide, turn, 0, unroll=wide)

    pitch = amp_c + 8

    def amp_chunk(chunk):
        amp_load(chunk).wait()
        for k in range(pairs):
            for h in range(virt // LANES):
                stage[h, k * pitch : k * pitch + amp_c, :] = raw[
                    chunk, k, :, h * LANES : (h + 1) * LANES
                ].astype(jnp.float32)
        for c in range(amp_c):
            for h in range(virt // LANES):
                amps[chunk * amp_c + c, :, h * LANES : (h + 1) * LANES] = stage[
                    h, pl.ds(c, pairs, stride=pitch), :
                ].astype(jnp.bfloat16)

    def integrals(first, count, steps):
        rows = left[first * wide * window : (first + count) * wide * window, :]
        for step in steps:
            for i in range(owned):
                side = right[flip_bits(z, step), i].reshape(virt, qs)
                at = (step * owned + i) * window
                ints[first * wide : (first + count) * wide, at : at + window, :] = (
                    lax.dot_general(
                        rows, side, (((1,), (1,)), ((), ())), preferred_element_type=jnp.float32
                    )
                    .astype(jnp.bfloat16)
                    .reshape(count * wide, window, virt)
                )

    def ladder(slab, steps):
        at, count = steps[0] * owned * window, len(steps) * owned * window
        span = range(slab * wide, (slab + 1) * wide)
        flat[at : at + count, :] += lax.dot_general(
            jnp.concatenate([ints[c, at : at + count, :] for c in span], axis=1),
            jnp.concatenate([amps[c] for c in span], axis=1),
            (((1,), (1,)), ((), ())),
            preferred_element_type=jnp.float32,
        )

    early, late = tuple(range(2)), tuple(range(2, nz))
    flat[...] = jnp.zeros_like(flat)
    own.wait()
    todo = list(range(chunks))

    def prepare(count=1):
        for chunk in todo[:count]:
            amp_chunk(chunk)
        del todo[:count]

    launch(0, range(1, nz))
    spread(factor_slab(0, z), 0, 0)
    prepare()
    for slab in range(1, slabs):
        launch(slab, (1,))
        spread(factor_slab(slab, z), slab, 0)
    prepare()
    for slab in range(1, slabs):
        launch(slab, late)
        prepare(slab % 2)
    for step in range(1, nz):
        from_z(0, step)
        prepare()
    for slab in range(1, slabs):
        from_z(slab, 1)
        from_x(slab - 1, 0)
        if slab > 1:
            prepare()
    prepare(chunks)
    from_x(slabs - 1, 0)
    for step in range(1, nz):
        from_x(0, step)
    for slab in range(1, slabs):
        from_x(slab, 1)

    def far_z(slab):
        if 0 < slab < slabs:
            for step in late:
                from_z(slab, step)

    def far_x(slab):
        if 0 < slab < slabs:
            for step in late:
                from_x(slab, step)

    far_z(1)
    for slab in range(slabs):
        make_left(slab)
        if slab == 0:
            from_core(early)
        integrals(slab, 1, early)
        if slab == 0:
            far_z(2)
        far_x(slab + 1)
        ladder(slab, early)
        if slab == 0:
            far_z(3)
    from_core(late)
    integrals(0, slabs, late)
    for slab in range(slabs):
        ladder(slab, late)

    for step in range(nz):
        for i in range(owned):
            at = (step * owned + i) * window
            acc[flip_bits(z, step) * owned + i] = flat[at : at + window, :]

    height = owned * split
    turns = split // owned
    here = z * nd + dev
    for at_z in range(nz):
        wide_row = jnp.concatenate([acc[at_z * owned + i] for i in range(owned)], axis=1)
        for at_d in range(nd):
            tiles_s[at_z, at_d] = wide_row[at_d * split : (at_d + 1) * split, :]
        for r in range(owned):
            turned = jnp.concatenate(
                [
                    acc[at_z * owned + r, pl.ds(i, window // owned, stride=owned), :]
                    for i in range(owned)
                ],
                axis=1,
            )
            for to_ba in range(window // owned):
                tiles_f[to_ba * nz + at_z, r : r + 1, :] = turned[to_ba : to_ba + 1, :]

    def post(source, target, at, to_ba, to_dev):
        there = to_ba * nd + to_dev

        @pl.when(there != me)
        def _():
            pltpu.make_async_remote_copy(
                src_ref=source,
                dst_ref=target,
                send_sem=sent_f.at[at],
                recv_sem=recv_f.at[at],
                device_id=(to_ba, to_dev),
                device_id_type=MESH,
            ).start()

        @pl.when(there == me)
        def _():
            pltpu.make_async_copy(source, target, recv_f.at[at]).start()

    def post_turned(to_ba, carry):
        for at_z in range(nz):
            owner = at_z * ny + y
            post(
                tiles_f.at[to_ba * nz + at_z],
                parts_f.at[owner % turns, here],
                1,
                to_ba,
                owner // turns,
            )
        return carry

    def post_straight(at_z, carry):
        for at_d in range(nd):
            post(tiles_s.at[at_z, at_d], parts_s.at[here], 0, at_z * ny + y, at_d)
        return carry

    if total <= 64:
        for to_ba in range(window // owned):
            if to_ba % ny == 0:
                post_straight(to_ba // ny, 0)
            post_turned(to_ba, 0)
    else:
        lax.fori_loop(0, nz, post_straight, 0)
        lax.fori_loop(0, window // owned, post_turned, 0)

    for copy in small:
        copy.wait()
    levels = to_column(levels_ref[...])
    level_at = lax.broadcasted_iota(jnp.int32, (levels.shape[0], window), 0)
    virtual = jnp.sum(
        jnp.where(level_at == vir_ref[...], levels, 0.0), axis=0, keepdims=True
    )
    level_occ = lax.broadcasted_iota(jnp.int32, (levels.shape[0], NOCC), 0)
    occupied = to_column(
        -jnp.sum(jnp.where(level_occ == occ_ref[...], levels, 0.0), axis=0, keepdims=True)
    )
    order = order_ref[...]
    first, second = order // NOCC, order % NOCC
    occ_at = lax.broadcasted_iota(jnp.int32, (NOCC, pairs), 0)
    pair_energy = jnp.sum(
        jnp.where(occ_at == first, occupied, 0.0), axis=0, keepdims=True
    ) + jnp.sum(jnp.where(occ_at == second, occupied, 0.0), axis=0, keepdims=True)
    win_row = lax.broadcasted_iota(jnp.int32, (height, window), 0)
    win_lane = lax.broadcasted_iota(jnp.int32, (height, window), 1)
    right_energy = jnp.sum(
        jnp.where(win_lane == ba * owned + win_row // split, virtual, 0.0), axis=1, keepdims=True
    )
    left_energy = jnp.sum(
        jnp.where(win_lane == dev * split + win_row % split, virtual, 0.0), axis=1, keepdims=True
    )
    denominator = right_energy + left_energy - pair_energy + level_shift
    permuter = (to_column(order) == second * NOCC + first).astype(jnp.float32)

    for at, place in enumerate((parts_s, parts_f)):
        pltpu.make_async_copy(place, place, recv_f.at[at]).wait()
    straight = jnp.sum(parts_s[...], axis=0)
    flipped = jnp.concatenate([jnp.sum(parts_f[j], axis=0) for j in range(turns)], axis=0)

    def stack(value):
        return jnp.concatenate(
            [value[:, i * pairs : (i + 1) * pairs] for i in range(owned)], axis=0
        )

    moved = jnp.dot(
        stack(flipped),
        permuter,
        precision=lax.Precision.HIGHEST,
        preferred_element_type=jnp.float32,
    )
    result = (stack(straight) + moved) / denominator
    for i in range(owned):
        for a in range(split):
            out_ref[i : i + 1, a * pairs : (a + 1) * pairs] = result[
                i * split + a : i * split + a + 1, :
            ]

    def await_sent(place, sem):
        pltpu.make_async_copy(place, place, sem).wait()

    await_sent(right.at[0 : nz - 1, :, 0], sent_z)
    await_sent(right.at[:, :, 0:no], sent_c)
    if no > 1:
        await_sent(right.at[:, :, 0 : no - 1], sent_x)
    if ny > 1:
        await_sent(other, sent_y)
    await_sent(parts_s.at[0 : nz * nd - 1], sent_f.at[0])
    kept = sum(
        jnp.where((at_z * ny + y) // turns == dev, 1, 0) for at_z in range(nz)
    )
    for count in range(2):

        @pl.when(kept == count)
        def _():
            await_sent(tiles_f.at[0 : tiles_f.shape[0] - count], sent_f.at[1])


def per_device(nba, ndev, factors, amplitudes, pair_order, occ_bin, vir_bin, levels):
    owned, cols, fitting = factors.shape
    pairs, _, virt = amplitudes.shape
    window = owned * nba
    ny = 1
    while ny * ny * 4 <= nba:
        ny *= 2
    nz = nba // ny
    no = ndev // 2
    qs = fitting // nz
    nb = nz * owned
    split = window // ndev
    amp_c = 16
    slabs = max(1, min(4, cols // 16))
    wide = cols // slabs
    dims = (nz, ny, no, owned, cols, qs, window, pairs, virt, amp_c, slabs)
    dma = pltpu.SemaphoreType.DMA
    vmem = pl.BlockSpec(memory_space=pltpu.VMEM)
    hbm = pl.BlockSpec(memory_space=pl.ANY)
    return pl.pallas_call(
        functools.partial(kernel, dims),
        out_shape=jax.ShapeDtypeStruct((owned, split * pairs), jnp.float32),
        in_specs=[hbm] * 6,
        out_specs=vmem,
        scratch_shapes=[
            pltpu.VMEM((1, pairs), jnp.int32),
            pltpu.VMEM((1, NOCC), jnp.int32),
            pltpu.VMEM((1, window), jnp.int32),
            pltpu.VMEM((1, levels.shape[0]), jnp.float32),
            pltpu.VMEM((nz, owned, ndev, cols, qs), jnp.bfloat16),
            pltpu.VMEM((slabs, max(1, ny - 1), nz, owned, wide, qs), jnp.bfloat16),
            pltpu.VMEM((qs // LANES, window * (wide + 8), LANES), jnp.float32),
            pltpu.VMEM((cols * window, qs), jnp.bfloat16),
            pltpu.VMEM((cols // amp_c, pairs, amp_c, virt), jnp.bfloat16),
            pltpu.VMEM((virt // LANES, pairs * (amp_c + 8), LANES), jnp.float32),
            pltpu.VMEM((cols, pairs, virt), jnp.bfloat16),
            pltpu.VMEM((cols, nb * window, virt), jnp.bfloat16),
            pltpu.VMEM((nb * window, pairs), jnp.float32),
            pltpu.VMEM((nb, window, pairs), jnp.float32),
            pltpu.VMEM((nz, ndev, split, owned * pairs), jnp.float32),
            pltpu.VMEM((nba * nz, owned, owned * pairs), jnp.float32),
            pltpu.VMEM((nz * ndev, split, owned * pairs), jnp.float32),
            pltpu.VMEM((split // owned, nz * ndev, owned, owned * pairs), jnp.float32),
            dma,
            dma((4,)),
            dma((cols // amp_c,)),
            dma,
            dma,
            dma,
            dma,
            dma((2,)),
            dma((slabs, nz - 1)),
            dma((slabs, nz, max(1, no - 1))),
            dma((2,)),
            dma((slabs,)),
            dma((2,)),
        ],
        compiler_params=pltpu.CompilerParams(
            collective_id=0,
            has_side_effects=True,
            vmem_limit_bytes=(63 if nb * window > 512 else 56) << 20,
        ),
    )(
        factors,
        amplitudes,
        pair_order.reshape(1, -1),
        occ_bin.reshape(1, -1),
        vir_bin.reshape(1, -1),
        levels.reshape(1, -1),
    )


def solution(mesh):
    return jax.shard_map(
        functools.partial(per_device, mesh.shape["ba"], mesh.shape["dev"]),
        mesh=mesh,
        in_specs=(P("ba", "dev", None), P(None, "dev", None), P(), P(), P(), P()),
        out_specs=P("ba", "dev"),
        check_vma=False,
    )
```

time: 41.6 us -> 37.8 us (0.909)
  Pallas kernels: 40.2 us -> 36.3 us
    pallas_call x1, Pallas kernels: 40.2 us -> 36.3 us  [per_device(): pl.pallas_call(functools.partial(kernel, dims), out_shape=jax.ShapeDtypeS...]
where the time goes in v2:
time: 37.8 us; the launch traced here: 37.6 us
  Pallas kernels  36.3 us (96%)
  local copies, waits for them, and re-layouts  1.26 us (3%)
    pallas_call x1, Pallas kernels, per_device(): pl.pallas_call(functools.partial(kernel, dims), out_shape=jax.ShapeDtypeS...  36.3 us
    unnamed x1, local copies, waits for them, and re-layouts  1.26 us

profile of v2, /device:TPU:0, one launch (start us, length us, event | category | flops | bytes accessed | tf_op | source)
XLA Modules:
  0.0 37.6 jit_solution(7901857593212967723)
XLA Ops:
  0.0 36.3 %shard_map.64 = f32[2,256]{1,0:T(2,128)} custom-call(bf16[2,128,1024]{2,1,0:T(8,128)(2,1)} %f_hbm.1, bf16[64,128,512]{2,1,0:T(8,128)(2,1)} %amps_hbm.1, s32[1,64]{1,0:T(1,128)} %bitcast.4, s32[1,8]{1,0:T(1,128)} %bitcast.5, s32[1,16]{1,0:T(1,128)} %bitcast.6, f32[1,128]{1,0:T(1,128)} %bitcast.7), custom_call_target="tpu_custom_call" | custom-call | tf_op jit(solution)/shard_map/pallas_call | solution.py:493
  36.3 1.3 %copy.8 = f32[2,256]{1,0:T(2,128)} copy(f32[2,256]{1,0:T(2,128)} %shard_map.64) | data formatting | bytes 4096

commit v3 on v2

--- a/solution.py
+++ b/solution.py
@@ -152,28 +152,32 @@
         at_z = flip_bits(z, step)
         send(source, piece(slab, at_z, at_d), sent_c, recv_c.at[min(step // 2, 1)], ba, partner_core)
 
-    def spread(source, slab, step):
-        at_z = flip_bits(z, step)
+    def source_of(slab, step):
+        return piece(slab, flip_bits(z, step), dev) if step else factor_slab(slab, z)
+
+    def spread_x(slab, step):
+        source = source_of(slab, step)
         for other_outer in range(1, no):
             send(
                 source,
-                piece(slab, at_z, dev),
+                piece(slab, flip_bits(z, step), dev),
                 sent_x,
                 recv_x.at[slab, step, other_outer - 1],
                 ba,
                 flip_bits(outer, other_outer) * 2 + core,
             )
+        to_partner(source, slab, step, dev)
+
+    def spread_y(slab, step):
         for other_y in range(1, ny):
             send(
-                source,
-                other.at[slab, other_y - 1, at_z],
+                source_of(slab, step),
+                other.at[slab, other_y - 1, flip_bits(z, step)],
                 sent_y,
                 recv_y.at[slab],
                 z * ny + flip_bits(y, other_y),
                 dev,
             )
-        to_partner(source, slab, step, dev)
-
 
     def launch(slab, steps):
         for step in steps:
@@ -187,10 +191,13 @@
                 dev,
             )
 
+    def land(slab, step):
+        await_bytes(piece(slab, flip_bits(z, step), dev), recv_z.at[slab, step - 1])
+
     def from_z(slab, step):
-        place = piece(slab, flip_bits(z, step), dev)
-        await_bytes(place, recv_z.at[slab, step - 1])
-        spread(place, slab, step)
+        land(slab, step)
+        spread_y(slab, step)
+        spread_x(slab, step)
 
     def from_x(slab, step):
         for other_outer in range(1, no):
@@ -272,8 +279,6 @@
         )
 
     early, late = tuple(range(2)), tuple(range(2, nz))
-    flat[...] = jnp.zeros_like(flat)
-    own.wait()
     todo = list(range(chunks))
 
     def prepare(count=1):
@@ -281,53 +286,89 @@
             amp_chunk(chunk)
         del todo[:count]
 
-    launch(0, range(1, nz))
-    spread(factor_slab(0, z), 0, 0)
+    @pl.when(core == 1)
+    def _():
+        flat[0:8, :] = lax.fori_loop(
+            0, 80, lambda at, value: value * 0.5 + 1.0, jnp.zeros((8, pairs), jnp.float32)
+        )
+
+    launch(0, (1,))
+    for slab in range(1, min(2, slabs)):
+        launch(slab, (1,))
+    spread_x(0, 0)
+    spread_y(0, 0)
+    launch(0, late[:-1])
     prepare()
-    for slab in range(1, slabs):
+    for slab in range(2, slabs):
         launch(slab, (1,))
-        spread(factor_slab(slab, z), slab, 0)
+        if slab == 2:
+            launch(0, late[-1:])
+        spread_x(slab - 1, 0)
+    if slabs < 3:
+        launch(0, late[-1:])
+    if slabs > 1:
+        spread_x(slabs - 1, 0)
+        spread_y(1, 0)
     prepare()
     for slab in range(1, slabs):
         launch(slab, late)
         prepare(slab % 2)
-    for step in range(1, nz):
-        from_z(0, step)
+    flat[...] = jnp.zeros_like(flat)
+    own.wait()
+    from_z(0, 1)
+    prepare()
+    if slabs > 1:
+        from_z(1, 1)
         prepare()
-    for slab in range(1, slabs):
-        from_z(slab, 1)
+    from_x(0, 0)
+    for step in late[:-1]:
+        land(0, step)
+        spread_y(0, step)
+        prepare()
+    for slab in range(2, slabs):
+        land(slab, 1)
+        spread_x(slab, 1)
         from_x(slab - 1, 0)
-        if slab > 1:
-            prepare()
+        prepare()
+    land(0, nz - 1)
+    spread_y(0, nz - 1)
+    if slabs > 1:
+        from_x(slabs - 1, 0)
+    for step in late:
+        spread_x(0, step)
+    for slab in range(2, slabs):
+        spread_y(slab, 0)
     prepare(chunks)
-    from_x(slabs - 1, 0)
-    for step in range(1, nz):
-        from_x(0, step)
-    for slab in range(1, slabs):
+    for slab in range(slabs):
         from_x(slab, 1)
 
     def far_z(slab):
         if 0 < slab < slabs:
             for step in late:
-                from_z(slab, step)
+                land(slab, step)
+                spread_y(slab, step)
+            for step in late:
+                spread_x(slab, step)
 
     def far_x(slab):
-        if 0 < slab < slabs:
+        if slab < slabs:
             for step in late:
                 from_x(slab, step)
 
     far_z(1)
+    for slab in range(2, slabs):
+        spread_y(slab, 1)
     for slab in range(slabs):
         make_left(slab)
         if slab == 0:
             from_core(early)
         integrals(slab, 1, early)
-        if slab == 0:
-            far_z(2)
-        far_x(slab + 1)
+        if slab > 1:
+            far_x(slab)
         ladder(slab, early)
-        if slab == 0:
-            far_z(3)
+        far_z(slab + 2)
+        if slab < 2:
+            far_x(slab)
     from_core(late)
     integrals(0, slabs, late)
     for slab in range(slabs):

time: 37.8 us -> 37 us (0.979)
  Pallas kernels: 36.3 us -> 35.6 us
    pallas_call x1, Pallas kernels: 36.3 us -> 35.6 us  [per_device(): pl.pallas_call(functools.partial(kernel, dims), out_shape=jax.ShapeDtypeS...]
where the time goes in v3:
time: 37 us; the launch traced here: 36.8 us
  Pallas kernels  35.6 us (96%)
  local copies, waits for them, and re-layouts  1.26 us (3%)
    pallas_call x1, Pallas kernels, per_device(): pl.pallas_call(functools.partial(kernel, dims), out_shape=jax.ShapeDtypeS...  35.6 us
    unnamed x1, local copies, waits for them, and re-layouts  1.26 us

profile of v3, /device:TPU:0, one launch (start us, length us, event | category | flops | bytes accessed | tf_op | source)
XLA Modules:
  0.0 36.8 jit_solution(13048871102744001912)
XLA Ops:
  0.0 35.6 %shard_map.64 = f32[2,256]{1,0:T(2,128)} custom-call(bf16[2,128,1024]{2,1,0:T(8,128)(2,1)} %f_hbm.1, bf16[64,128,512]{2,1,0:T(8,128)(2,1)} %amps_hbm.1, s32[1,64]{1,0:T(1,128)} %bitcast.4, s32[1,8]{1,0:T(1,128)} %bitcast.5, s32[1,16]{1,0:T(1,128)} %bitcast.6, f32[1,128]{1,0:T(1,128)} %bitcast.7), custom_call_target="tpu_custom_call" | custom-call | tf_op jit(solution)/shard_map/pallas_call | solution.py:534
  35.6 1.3 %copy.8 = f32[2,256]{1,0:T(2,128)} copy(f32[2,256]{1,0:T(2,128)} %shard_map.64) | data formatting | bytes 4096

commit v4 on v3

--- a/solution.py
+++ b/solution.py
@@ -340,6 +340,13 @@
         spread_y(slab, 0)
     prepare(chunks)
     for slab in range(slabs):
+        if slabs > 1 and slab == slabs - 2:
+            for step in late[:-1]:
+                land(1, step)
+                spread_y(1, step)
+        if slabs > 1 and slab == slabs - 1:
+            land(1, nz - 1)
+            spread_y(1, nz - 1)
         from_x(slab, 1)
 
     def far_z(slab):
@@ -355,7 +362,9 @@
             for step in late:
                 from_x(slab, step)
 
-    far_z(1)
+    if slabs > 1:
+        for step in late:
+            spread_x(1, step)
     for slab in range(2, slabs):
         spread_y(slab, 1)
     for slab in range(slabs):
@@ -365,8 +374,8 @@
         integrals(slab, 1, early)
         if slab > 1:
             far_x(slab)
+        far_z(slab + 2)
         ladder(slab, early)
-        far_z(slab + 2)
         if slab < 2:
             far_x(slab)
     from_core(late)

time: 37 us -> 36.6 us (0.989)
  Pallas kernels: 35.6 us -> 35.2 us
    pallas_call x1, Pallas kernels: 35.6 us -> 35.2 us  [per_device(): pl.pallas_call(functools.partial(kernel, dims), out_shape=jax.ShapeDtypeS...]
where the time goes in v4:
time: 36.6 us; the launch traced here: 36.4 us
  Pallas kernels  35.2 us (96%)
  local copies, waits for them, and re-layouts  1.26 us (3%)
    pallas_call x1, Pallas kernels, per_device(): pl.pallas_call(functools.partial(kernel, dims), out_shape=jax.ShapeDtypeS...  35.2 us
    unnamed x1, local copies, waits for them, and re-layouts  1.26 us

profile of v4, /device:TPU:0, one launch (start us, length us, event | category | flops | bytes accessed | tf_op | source)
XLA Modules:
  0.0 36.4 jit_solution(12052121147138046539)
XLA Ops:
  0.0 35.2 %shard_map.64 = f32[2,256]{1,0:T(2,128)} custom-call(bf16[2,128,1024]{2,1,0:T(8,128)(2,1)} %f_hbm.1, bf16[64,128,512]{2,1,0:T(8,128)(2,1)} %amps_hbm.1, s32[1,64]{1,0:T(1,128)} %bitcast.4, s32[1,8]{1,0:T(1,128)} %bitcast.5, s32[1,16]{1,0:T(1,128)} %bitcast.6, f32[1,128]{1,0:T(1,128)} %bitcast.7), custom_call_target="tpu_custom_call" | custom-call | tf_op jit(solution)/shard_map/pallas_call | solution.py:543
  35.2 1.3 %copy.8 = f32[2,256]{1,0:T(2,128)} copy(f32[2,256]{1,0:T(2,128)} %shard_map.64) | data formatting | bytes 4096

commit v5 on v3

--- a/solution.py
+++ b/solution.py
@@ -365,8 +365,8 @@
         integrals(slab, 1, early)
         if slab > 1:
             far_x(slab)
+        far_z(slab + 2)
         ladder(slab, early)
-        far_z(slab + 2)
         if slab < 2:
             far_x(slab)
     from_core(late)

time: 37 us -> 36.5 us (0.986)
  Pallas kernels: 35.6 us -> 35 us
    pallas_call x1, Pallas kernels: 35.6 us -> 35 us  [per_device(): pl.pallas_call(functools.partial(kernel, dims), out_shape=jax.ShapeDtypeS...]
where the time goes in v5:
time: 36.5 us; the launch traced here: 36.3 us
  Pallas kernels  35 us (96%)
  local copies, waits for them, and re-layouts  1.26 us (3%)
    pallas_call x1, Pallas kernels, per_device(): pl.pallas_call(functools.partial(kernel, dims), out_shape=jax.ShapeDtypeS...  35 us
    unnamed x1, local copies, waits for them, and re-layouts  1.26 us

profile of v5, /device:TPU:0, one launch (start us, length us, event | category | flops | bytes accessed | tf_op | source)
XLA Modules:
  0.0 36.3 jit_solution(15638903797331270224)
XLA Ops:
  0.0 35.0 %shard_map.64 = f32[2,256]{1,0:T(2,128)} custom-call(bf16[2,128,1024]{2,1,0:T(8,128)(2,1)} %f_hbm.1, bf16[64,128,512]{2,1,0:T(8,128)(2,1)} %amps_hbm.1, s32[1,64]{1,0:T(1,128)} %bitcast.4, s32[1,8]{1,0:T(1,128)} %bitcast.5, s32[1,16]{1,0:T(1,128)} %bitcast.6, f32[1,128]{1,0:T(1,128)} %bitcast.7), custom_call_target="tpu_custom_call" | custom-call | tf_op jit(solution)/shard_map/pallas_call | solution.py:534
  35.0 1.3 %copy.8 = f32[2,256]{1,0:T(2,128)} copy(f32[2,256]{1,0:T(2,128)} %shard_map.64) | data formatting | bytes 4096
